TPU v7x, 32 devices: a whole 2x2x4 slice. The times are simulated.
32 devices in a mesh: macro: 8 (over z, x), rep: 4 (over y, core).
Axes of the slice: x: 2, y: 2, z: 4, core: 2. Of those that a mesh axis runs over, the one named last changes fastest.
Arguments:
- u_old: float32 [4096], P('macro'), may hold values from -1 to 1
- coarse_kinetic_speed: float32 [4096], P('macro'), may hold values from 0.2 to 3
- micro_spreading_coefficient: float32 [4096], P('macro'), may hold values from 0.08 to 0.4
- micro_seed: int32 [4, 4096, 256], P('rep', 'macro'), may hold values from 0 to 1073741823
Outputs:
- new_state: float32 [4096], P('macro')
All inputs are finite; a program needn't handle non-finite values.
Results may differ from a plain program's by a relative error of at most 0.0001.
Values sent between devices are 32-bit elements; how exact they have to be, the bound alone decides.
A program may use at most 64 MiB of HBM per device.

v0:
```python
import math

import jax
import jax.numpy as jnp
from jax import lax
from jax.sharding import PartitionSpec as P

STEPS = 8
ITERS = 4


noise_amp = 1.0
micro_dt = 0.02
proj_step = 0.25
fd_step = 0.01
seed_scale = 2.0 ** (-30)


def with_halo(cells, sides, width):
    for axis, dim in sides:
        count = lax.axis_size(axis)
        ends = count - 1
        head = lax.slice_in_dim(cells, 0, width, axis=dim)
        tail = lax.slice_in_dim(cells, cells.shape[dim] - width, cells.shape[dim], axis=dim)
        cells = jnp.concatenate(
            [
                lax.ppermute(tail, axis, [(i, (i + 1) % count) for i in range(ends)]),
                cells,
                lax.ppermute(head, axis, [((i + 1) % count, i) for i in range(ends)]),
            ],
            axis=dim,
        )
    return cells


def lifted(padded_density, cells):
    left = padded_density[:-2]
    centre = padded_density[1:-1]
    right = padded_density[2:]
    slope = 0.5 * (right - left)
    bend = 0.5 * (right - 2.0 * centre + left)
    place = (jnp.arange(cells).astype(jnp.float32) + 0.5) / cells - 0.5
    inside = (
        centre[:, None] + slope[:, None] * place[None, :] + bend[:, None] * (place * place)[None, :]
    )
    edge = 0.5 + 0.5 / cells
    ghost_left = centre - slope * edge + bend * edge * edge
    ghost_right = centre + slope * edge + bend * edge * edge
    return (inside, ghost_left, ghost_right)


def ensemble_aggregate(padded_density, pointwise_kinetic_speed, spreading_current, stochastic_kick):
    inside, ghost_left, ghost_right = lifted(padded_density, stochastic_kick.shape[2])
    start = inside[None] + stochastic_kick
    left_col = ghost_left[None, :, None]
    right_col = ghost_right[None, :, None]
    kappa = spreading_current[None, :, None]
    growth = micro_dt * pointwise_kinetic_speed[None, :, None]
    state = start
    for step in range(STEPS):
        upper = jnp.concatenate([state[:, :, 1:], right_col], axis=2)
        lower = jnp.concatenate([left_col, state[:, :, :-1]], axis=2)
        state = (
            state + kappa * (upper + lower - 2.0 * state) + growth * (state - state * state * state)
        )
    return jnp.sum(state - start, axis=(0, 2))


def least_squares(hess, beta, iters):
    target = [beta] + [beta * 0.0 for index in range(iters)]
    cosines = []
    sines = []
    upper = []
    for col_index in range(iters):
        column = [hess[row][col_index] for row in range(col_index + 2)]
        for row in range(col_index):
            first = column[row]
            second = column[row + 1]
            column[row] = cosines[row] * first + sines[row] * second
            column[row + 1] = -sines[row] * first + cosines[row] * second
        radius = jnp.sqrt(
            column[col_index] * column[col_index] + column[col_index + 1] * column[col_index + 1]
        )
        cosine = column[col_index] / radius
        sine = column[col_index + 1] / radius
        cosines.append(cosine)
        sines.append(sine)
        column[col_index] = radius
        upper.append(column[: col_index + 1])
        head = target[col_index]
        target[col_index] = cosine * head
        target[col_index + 1] = -sine * head
    solved = [None] * iters
    for row in range(iters - 1, -1, -1):
        acc = target[row]
        for later in range(row + 1, iters):
            acc = acc - upper[later][row] * solved[later]
        solved[row] = acc / upper[row][row]
    return solved


def per_device(u_old, coarse_kinetic_speed, micro_spreading_coefficient, micro_seed):
    local = u_old.shape[0]
    groups = lax.axis_size("rep")
    fluctuation_amplitude = 1.0 / (
        micro_seed.shape[0] * groups * micro_seed.shape[2] * STEPS * micro_dt
    )
    delta = fd_step * math.sqrt(lax.axis_size("macro") * local)
    stochastic_kick = noise_amp * (micro_seed.astype(jnp.float32) * seed_scale - 0.5)

    def drift(species_density):
        padded_density = with_halo(species_density, (("macro", 0),), 1)
        increment_parts = ensemble_aggregate(
            padded_density, coarse_kinetic_speed, micro_spreading_coefficient, stochastic_kick
        )
        summed = lax.psum(increment_parts, "rep")
        return summed * fluctuation_amplitude

    def inner(values):
        return lax.psum(values, "macro")

    f_old = drift(u_old)
    u_start = u_old + proj_step * f_old
    f_start = drift(u_start)
    resid = -(u_start - u_old - proj_step * f_start)
    beta = jnp.sqrt(inner(jnp.sum(resid * resid)))
    basis = [resid / beta]
    hess = [[None] * ITERS for row in range(ITERS + 1)]
    for col_index in range(ITERS):
        probe = basis[col_index]
        image = probe - proj_step * (drift(u_start + delta * probe) - f_start) / delta
        pieces = [jnp.sum(basis[row] * image) for row in range(col_index + 1)]
        pieces.append(jnp.sum(image * image))
        dots = inner(jnp.stack(pieces))
        for row in range(col_index + 1):
            hess[row][col_index] = dots[row]
            image = image - dots[row] * basis[row]
        coeff_sq = jnp.sum(dots[: col_index + 1] * dots[: col_index + 1])
        length = jnp.sqrt(jnp.maximum(dots[col_index + 1] - coeff_sq, 0.0))
        hess[col_index + 1][col_index] = length
        basis.append(image / length)
    coeffs = least_squares(hess, beta, ITERS)
    result = u_start
    for col_index in range(ITERS):
        result = result + coeffs[col_index] * basis[col_index]
    return result


def solution(mesh):
    placed = (P("macro"), P("macro"), P("macro"), P("rep", "macro", None))
    return jax.shard_map(
        per_device, mesh=mesh, in_specs=placed, out_specs=P("macro"), check_vma=False
    )
```

profile of v0, /device:TPU:0, one launch (start us, length us, event | category | flops | bytes accessed | tf_op | source)
XLA Modules:
  0.0 276.7 jit_solution(14354860609766797719)
XLA Ops:
  0.0 1.4 fusion.354
  1.4 1.4 collective-permute-start
  2.8 6.0 %collective-permute-start.1 = (f32[1]{0:T(128)}, f32[1]{0:T(128)}, u32[]{:S(2)}, u32[]{:S(2)}) collective-permute-start(f32[1]{0:T(128)} %get-tuple-element.172), channel_id=1, source_target_pairs={{0,4},{4,8},{8,12},{12,16},{16,20},{20,24},{24,28},{1,5},{5,9},{9,... | collective-permute-start | bytes 20 | tf_op jit(solution)/shard_map/ppermute | solution.py:27
  18.9 6.5 %psum.77 = f32[512]{0:T(512)S(1)} all-reduce(f32[512]{0:T(512)S(1)} %fusion.17), channel_id=1, replica_groups=mesh['macro'=8,'rep'=4] {'rep'}, use_global_device_ids=true, to_apply=%region_1.0 | all-reduce | flops 512 | bytes 4096 | tf_op jit(solution)/shard_map/psum | solution.py:116
  27.4 5.2 %collective-permute-start.3 = (f32[1]{0:T(128)}, f32[1]{0:T(128)}, u32[]{:S(2)}, u32[]{:S(2)}) collective-permute-start(f32[1]{0:T(128)} %get-tuple-element.168), channel_id=1, source_target_pairs={{0,4},{4,8},{8,12},{12,16},{16,20},{20,24},{24,28},{1,5},{5,9},{9,... | collective-permute-start | bytes 20 | tf_op jit(solution)/shard_map/ppermute | solution.py:27
  40.8 5.9 %psum.78 = f32[512]{0:T(512)S(1)} all-reduce(f32[512]{0:T(512)S(1)} %fusion.35), channel_id=1, replica_groups=mesh['macro'=8,'rep'=4] {'rep'}, use_global_device_ids=true, to_apply=%region_3.0 | all-reduce | flops 512 | bytes 4096 | tf_op jit(solution)/shard_map/psum | solution.py:116
  47.4 25.6 %psum.79 = f32[]{:T(128)} all-reduce(f32[]{:T(128)} %multiply_reduce_fusion.14), channel_id=1, replica_groups=mesh['macro'=8,'rep'=4] {'macro'}, use_global_device_ids=true, to_apply=%region_5.0 | all-reduce | flops 1 | bytes 8 | tf_op jit(solution)/shard_map/psum | solution.py:120
  75.7 5.1 %collective-permute-start.5 = (f32[1]{0:T(128)}, f32[1]{0:T(128)}, u32[]{:S(2)}, u32[]{:S(2)}) collective-permute-start(f32[1]{0:T(128)} %get-tuple-element.164), channel_id=1, source_target_pairs={{0,4},{4,8},{8,12},{12,16},{16,20},{20,24},{24,28},{1,5},{5,9},{9,... | collective-permute-start | bytes 20 | tf_op jit(solution)/shard_map/ppermute | solution.py:27
  89.0 5.7 %psum.80 = f32[512]{0:T(512)S(1)} all-reduce(f32[512]{0:T(512)S(1)} %fusion.53), channel_id=1, replica_groups=mesh['macro'=8,'rep'=4] {'rep'}, use_global_device_ids=true, to_apply=%region_7.0 | all-reduce | flops 512 | bytes 4096 | tf_op jit(solution)/shard_map/psum | solution.py:116
  95.4 1.4 pad_maximum_fusion.108
  96.8 19.5 %psum.81 = f32[2]{0:T(128)S(1)} all-reduce(f32[2]{0:T(128)S(1)} %pad_maximum_fusion.108), channel_id=1, replica_groups=mesh['macro'=8,'rep'=4] {'macro'}, use_global_device_ids=true, to_apply=%region_10.0 | all-reduce | flops 2 | bytes 16 | tf_op jit(solution)/shard_map/psum | solution.py:120
  123.6 5.1 %collective-permute-start.7 = (f32[1]{0:T(128)}, f32[1]{0:T(128)}, u32[]{:S(2)}, u32[]{:S(2)}) collective-permute-start(f32[1]{0:T(128)} %get-tuple-element.160), channel_id=1, source_target_pairs={{0,4},{4,8},{8,12},{12,16},{16,20},{20,24},{24,28},{1,5},{5,9},{9,... | collective-permute-start | bytes 20 | tf_op jit(solution)/shard_map/ppermute | solution.py:27
  137.0 5.7 %psum.82 = f32[512]{0:T(512)S(1)} all-reduce(f32[512]{0:T(512)S(1)} %fusion.71), channel_id=1, replica_groups=mesh['macro'=8,'rep'=4] {'rep'}, use_global_device_ids=true, to_apply=%region_12.0 | all-reduce | flops 512 | bytes 4096 | tf_op jit(solution)/shard_map/psum | solution.py:116
  143.4 2.0 pad_maximum_fusion.109
  145.3 19.5 %psum.83 = f32[3]{0:T(128)S(1)} all-reduce(f32[3]{0:T(128)S(1)} %pad_maximum_fusion.109), channel_id=1, replica_groups=mesh['macro'=8,'rep'=4] {'macro'}, use_global_device_ids=true, to_apply=%region_16.0 | all-reduce | flops 3 | bytes 24 | tf_op jit(solution)/shard_map/psum | solution.py:120
  173.5 5.1 %collective-permute-start.9 = (f32[1]{0:T(128)}, f32[1]{0:T(128)}, u32[]{:S(2)}, u32[]{:S(2)}) collective-permute-start(f32[1]{0:T(128)} %get-tuple-element.156), channel_id=1, source_target_pairs={{0,4},{4,8},{8,12},{12,16},{16,20},{20,24},{24,28},{1,5},{5,9},{9,... | collective-permute-start | bytes 20 | tf_op jit(solution)/shard_map/ppermute | solution.py:27
  186.8 5.7 %psum.84 = f32[512]{0:T(512)S(1)} all-reduce(f32[512]{0:T(512)S(1)} %fusion.89), channel_id=1, replica_groups=mesh['macro'=8,'rep'=4] {'rep'}, use_global_device_ids=true, to_apply=%region_19.0 | all-reduce | flops 512 | bytes 4096 | tf_op jit(solution)/shard_map/psum | solution.py:116
  193.2 2.6 pad_maximum_fusion.110
  195.8 19.5 %psum.85 = f32[4]{0:T(128)S(1)} all-reduce(f32[4]{0:T(128)S(1)} %pad_maximum_fusion.110), channel_id=1, replica_groups=mesh['macro'=8,'rep'=4] {'macro'}, use_global_device_ids=true, to_apply=%region_24.0 | all-reduce | flops 4 | bytes 32 | tf_op jit(solution)/shard_map/psum | solution.py:120
  221.9 1.9 multiply_add_fusion.2
  225.7 5.1 %collective-permute-start.11 = (f32[1]{0:T(128)}, f32[1]{0:T(128)}, u32[]{:S(2)}, u32[]{:S(2)}) collective-permute-start(f32[1]{0:T(128)} %get-tuple-element.152), channel_id=1, source_target_pairs={{0,4},{4,8},{8,12},{12,16},{16,20},{20,24},{24,28},{1,5},{5,9},{9,... | collective-permute-start | bytes 20 | tf_op jit(solution)/shard_map/ppermute | solution.py:27
  239.1 5.7 %psum.86 = f32[512]{0:T(512)S(1)} all-reduce(f32[512]{0:T(512)S(1)} %fusion.107), channel_id=1, replica_groups=mesh['macro'=8,'rep'=4] {'rep'}, use_global_device_ids=true, to_apply=%region_27.0 | all-reduce | flops 512 | bytes 4096 | tf_op jit(solution)/shard_map/psum | solution.py:116
  245.5 3.2 %stack.71 = f32[5]{0:T(128)S(1)} concatenate(f32[1]{0:T(128)} %bitcast.30, f32[1]{0:T(128)} %bitcast.31, f32[1]{0:T(128)} %bitcast.32, f32[1]{0:T(128)} %bitcast.33, f32[1]{0:T(128)} %bitcast.34), dimensions={0} | concatenate | bytes 40 | tf_op jit(solution)/shard_map/stack | solution.py:134
  248.7 19.5 %psum.87 = f32[5]{0:T(128)S(1)} all-reduce(f32[5]{0:T(128)S(1)} %stack.71), channel_id=1, replica_groups=mesh['macro'=8,'rep'=4] {'macro'}, use_global_device_ids=true, to_apply=%region_33.0 | all-reduce | flops 5 | bytes 40 | tf_op jit(solution)/shard_map/psum | solution.py:120
  (175 shorter events, 71.3 us)
Async XLA Ops:
  1.4 7.5 %copy-start.3 = (f32[512]{0:T(512)S(1)}, f32[512]{0:T(512)}, u32[]{:S(2)}) copy-start(f32[512]{0:T(512)} %param.5) | copy-start | bytes 6148
  1.4 7.5 %collective-permute-start = (f32[1]{0:T(128)}, f32[1]{0:T(128)}, u32[]{:S(2)}, u32[]{:S(2)}) collective-permute-start(f32[1]{0:T(128)} %get-tuple-element.171), channel_id=1, source_target_pairs={{4,0},{8,4},{12,8},{16,12},{20,16},{24,20},{28,24},{5,1},{9,5},{13... | collective-permute-start | bytes 20 | tf_op jit(solution)/shard_map/ppermute | solution.py:29
  2.8 6.8 %collective-permute-start.1 = (f32[1]{0:T(128)}, f32[1]{0:T(128)}, u32[]{:S(2)}, u32[]{:S(2)}) collective-permute-start(f32[1]{0:T(128)} %get-tuple-element.172), channel_id=1, source_target_pairs={{0,4},{4,8},{8,12},{12,16},{16,20},{20,24},{24,28},{1,5},{5,9},{9,... | collective-permute-start | bytes 20 | tf_op jit(solution)/shard_map/ppermute | solution.py:27
  8.9 0.8 copy-start.2
  12.5 1.0 copy-start
  12.9 0.7 copy-start.1
  26.1 6.5 %collective-permute-start.2 = (f32[1]{0:T(128)}, f32[1]{0:T(128)}, u32[]{:S(2)}, u32[]{:S(2)}) collective-permute-start(f32[1]{0:T(128)} %get-tuple-element.167), channel_id=1, source_target_pairs={{4,0},{8,4},{12,8},{16,12},{20,16},{24,20},{28,24},{5,1},{9,5},{13... | collective-permute-start | bytes 20 | tf_op jit(solution)/shard_map/ppermute | solution.py:29
  27.4 6.0 %collective-permute-start.3 = (f32[1]{0:T(128)}, f32[1]{0:T(128)}, u32[]{:S(2)}, u32[]{:S(2)}) collective-permute-start(f32[1]{0:T(128)} %get-tuple-element.168), channel_id=1, source_target_pairs={{0,4},{4,8},{8,12},{12,16},{16,20},{20,24},{24,28},{1,5},{5,9},{9,... | collective-permute-start | bytes 20 | tf_op jit(solution)/shard_map/ppermute | solution.py:27
  74.4 6.4 %collective-permute-start.4 = (f32[1]{0:T(128)}, f32[1]{0:T(128)}, u32[]{:S(2)}, u32[]{:S(2)}) collective-permute-start(f32[1]{0:T(128)} %get-tuple-element.163), channel_id=1, source_target_pairs={{4,0},{8,4},{12,8},{16,12},{20,16},{24,20},{28,24},{5,1},{9,5},{13... | collective-permute-start | bytes 20 | tf_op jit(solution)/shard_map/ppermute | solution.py:29
  75.7 5.9 %collective-permute-start.5 = (f32[1]{0:T(128)}, f32[1]{0:T(128)}, u32[]{:S(2)}, u32[]{:S(2)}) collective-permute-start(f32[1]{0:T(128)} %get-tuple-element.164), channel_id=1, source_target_pairs={{0,4},{4,8},{8,12},{12,16},{16,20},{20,24},{24,28},{1,5},{5,9},{9,... | collective-permute-start | bytes 20 | tf_op jit(solution)/shard_map/ppermute | solution.py:27
  122.3 6.4 %collective-permute-start.6 = (f32[1]{0:T(128)}, f32[1]{0:T(128)}, u32[]{:S(2)}, u32[]{:S(2)}) collective-permute-start(f32[1]{0:T(128)} %get-tuple-element.159), channel_id=1, source_target_pairs={{4,0},{8,4},{12,8},{16,12},{20,16},{24,20},{28,24},{5,1},{9,5},{13... | collective-permute-start | bytes 20 | tf_op jit(solution)/shard_map/ppermute | solution.py:29
  123.6 5.9 %collective-permute-start.7 = (f32[1]{0:T(128)}, f32[1]{0:T(128)}, u32[]{:S(2)}, u32[]{:S(2)}) collective-permute-start(f32[1]{0:T(128)} %get-tuple-element.160), channel_id=1, source_target_pairs={{0,4},{4,8},{8,12},{12,16},{16,20},{20,24},{24,28},{1,5},{5,9},{9,... | collective-permute-start | bytes 20 | tf_op jit(solution)/shard_map/ppermute | solution.py:27
  172.2 6.4 %collective-permute-start.8 = (f32[1]{0:T(128)}, f32[1]{0:T(128)}, u32[]{:S(2)}, u32[]{:S(2)}) collective-permute-start(f32[1]{0:T(128)} %get-tuple-element.155), channel_id=1, source_target_pairs={{4,0},{8,4},{12,8},{16,12},{20,16},{24,20},{28,24},{5,1},{9,5},{13... | collective-permute-start | bytes 20 | tf_op jit(solution)/shard_map/ppermute | solution.py:29
  173.5 5.9 %collective-permute-start.9 = (f32[1]{0:T(128)}, f32[1]{0:T(128)}, u32[]{:S(2)}, u32[]{:S(2)}) collective-permute-start(f32[1]{0:T(128)} %get-tuple-element.156), channel_id=1, source_target_pairs={{0,4},{4,8},{8,12},{12,16},{16,20},{20,24},{24,28},{1,5},{5,9},{9,... | collective-permute-start | bytes 20 | tf_op jit(solution)/shard_map/ppermute | solution.py:27
  224.4 6.4 %collective-permute-start.10 = (f32[1]{0:T(128)}, f32[1]{0:T(128)}, u32[]{:S(2)}, u32[]{:S(2)}) collective-permute-start(f32[1]{0:T(128)} %get-tuple-element.151), channel_id=1, source_target_pairs={{4,0},{8,4},{12,8},{16,12},{20,16},{24,20},{28,24},{5,1},{9,5},{13... | collective-permute-start | bytes 20 | tf_op jit(solution)/shard_map/ppermute | solution.py:29
  225.7 5.9 %collective-permute-start.11 = (f32[1]{0:T(128)}, f32[1]{0:T(128)}, u32[]{:S(2)}, u32[]{:S(2)}) collective-permute-start(f32[1]{0:T(128)} %get-tuple-element.152), channel_id=1, source_target_pairs={{0,4},{4,8},{8,12},{12,16},{16,20},{20,24},{24,28},{1,5},{5,9},{9,... | collective-permute-start | bytes 20 | tf_op jit(solution)/shard_map/ppermute | solution.py:27
where the time goes:
time: 278 us; the launch traced here: 277 us
  blocking collectives  139 us (50%)
  other arithmetic  49.8 us (18%)
  starting transfers between devices  39.4 us (14%)
  local copies, waits for them, and re-layouts  22.8 us (8%)
  between operations  21.2 us (8%)
  waiting for transfers between devices  4.81 us (2%)
    psum x5, blocking collectives, inner(): return lax.psum(values, 'macro')  104 us
    psum x6, blocking collectives, drift(): summed = lax.psum(increment_parts, 'rep')  35.1 us
    ppermute x6, starting transfers between devices, with_halo(): lax.ppermute(tail, axis, [(i, (i + 1) % count) for i in range(ends)])  31.6 us
    add x42, other arithmetic, ensemble_aggregate(): state + kappa * (upper + lower - 2.0 * state)  18.7 us
    slice x48, local copies, waits for them, and re-layouts, ensemble_aggregate(): lower = jnp.concatenate([left_col, state[:, :, :-1]], axis=2)  9.65 us
    ppermute x6, starting transfers between devices, with_halo(): lax.ppermute(head, axis, [((i + 1) % count, i) for i in range(ends)])  7.81 us
    concatenate x6, other arithmetic, with_halo(): jnp.concatenate([lax.ppermute(tail, axis, [(i, (i + 1) % count) for i in...  7.59 us
    another operation x3, other arithmetic, per_device(): dots = inner(jnp.stack(pieces))  5.98 us
  transfers between devices with their start and end apart: 12, of which 6 were waited for; matrix products, arithmetic and copies ran while one was open for 0% of the time, Pallas kernels for 0%

commit v1 on v0

v1 whole, which is shorter than its diff:
```python
import functools
import math

import jax
import jax.numpy as jnp
from jax import lax
from jax.experimental import pallas as pl
from jax.experimental.pallas import tpu as pltpu
from jax.sharding import PartitionSpec as P

STEPS = 8
ITERS = 4
LANES = 128
SUB = 8

noise_amp = 1.0
micro_dt = 0.02
proj_step = 0.25
fd_step = 0.01
seed_scale = 2.0 ** (-30)

MESH = pl.DeviceIdType.MESH


def total(values):
    return jnp.sum(jnp.sum(values, axis=0, keepdims=True), axis=1, keepdims=True)


class Givens:
    def __init__(self, beta):
        self.target = [beta]
        self.cosines = []
        self.sines = []
        self.upper = []

    def add(self, column):
        column = list(column)
        last = len(column) - 2
        for row in range(last):
            first, second = column[row], column[row + 1]
            column[row] = self.cosines[row] * first + self.sines[row] * second
            column[row + 1] = -self.sines[row] * first + self.cosines[row] * second
        radius = jnp.sqrt(column[last] * column[last] + column[last + 1] * column[last + 1])
        cosine = column[last] / radius
        sine = column[last + 1] / radius
        self.cosines.append(cosine)
        self.sines.append(sine)
        column[last] = radius
        self.upper.append(column[: last + 1])
        head = self.target[last]
        self.target[last] = cosine * head
        self.target.append(-sine * head)

    def solve(self):
        count = len(self.upper)
        solved = [None] * count
        for row in range(count - 1, -1, -1):
            acc = self.target[row]
            for later in range(row + 1, count):
                acc = acc - self.upper[later][row] * solved[later]
            solved[row] = acc / self.upper[row][row]
        return solved


def kernel(
    macros,
    reps,
    cells,
    rows,
    u_ref,
    rate_ref,
    kappa_ref,
    seed_ref,
    out_ref,
    raw,
    flipped,
    noise,
    noise_sum,
    coefs,
    parts,
    whole,
    load_sem,
    part_send,
    part_recv,
    whole_send,
    whole_recv,
):
    depth = cells // SUB
    pitch = flipped.shape[0] // SUB
    me = lax.axis_index("macro")
    rep = lax.axis_index("rep")
    local = rows * LANES
    amplitude = 1.0 / (reps * cells * STEPS * micro_dt)
    delta = fd_step * math.sqrt(macros * local)

    loads = [
        pltpu.make_async_copy(
            seed_ref.at[0, pl.ds(g * LANES, LANES), :], raw.at[g], load_sem.at[g]
        )
        for g in range(rows)
    ]
    for load in loads:
        load.start()

    barrier = pltpu.get_barrier_semaphore()
    for d in range(1, macros):
        pl.semaphore_signal(
            barrier, inc=1, device_id={"macro": lax.rem(me + d, macros)}, device_id_type=MESH
        )
    for d in range(1, reps):
        pl.semaphore_signal(
            barrier, inc=1, device_id={"rep": lax.rem(rep + d, reps)}, device_id_type=MESH
        )

    growth = micro_dt * rate_ref[...]
    scale = jnp.sqrt(growth)
    kappa = kappa_ref[...]
    coefs[5] = kappa
    coefs[6] = 1.0 + growth - 2.0 * kappa
    coefs[7] = 1.0 + growth
    unscale = 1.0 / scale
    coefs[8] = unscale
    coefs[9] = scale

    def row(index, g):
        return jnp.broadcast_to(coefs[index, pl.ds(g, 1), :], (SUB, LANES))

    for load in loads:
        load.wait()

    def prepare(g, carry):
        values = raw[g].astype(jnp.float32).T
        for s in range(SUB):
            flipped[s * pitch : s * pitch + depth, :] = values[s * depth : (s + 1) * depth]
        factor = row(9, g)
        acc = None
        for k in range(depth):
            kick = noise_amp * (flipped[pl.ds(k, SUB, stride=pitch), :] * seed_scale - 0.5)
            acc = kick if acc is None else acc + kick
            noise[g, k] = factor * kick
        noise_sum[pl.ds(g, 1), :] = jnp.sum(acc, axis=0, keepdims=True)
        return carry

    lax.fori_loop(0, rows, prepare, 0)

    pl.semaphore_wait(barrier, macros - 1 + reps - 1)

    lane = lax.broadcasted_iota(jnp.int32, (rows, LANES), 1)
    sub = lax.broadcasted_iota(jnp.int32, (SUB, LANES), 0)
    places = [(c + 0.5) / cells - 0.5 for c in range(cells)]
    square_sum = sum(x * x for x in places)
    first_place = sub.astype(jnp.float32) * (depth / cells) + (0.5 / cells - 0.5)
    edge = 0.5 + 0.5 / cells

    def send_whole(r, source, ds):
        copies = []
        for d in ds:
            copy = pltpu.make_async_remote_copy(
                src_ref=source,
                dst_ref=whole.at[r, d],
                send_sem=whole_send.at[r, d],
                recv_sem=whole_recv.at[r, d],
                device_id={"macro": lax.rem(me + (macros - d), macros)},
                device_id_type=MESH,
            )
            copy.start()
            copies.append(copy)
        return copies

    def send_parts(i):
        copies = []
        for d in range(1, reps):
            copy = pltpu.make_async_remote_copy(
                src_ref=parts.at[i, rep],
                dst_ref=parts.at[i, rep],
                send_sem=part_send.at[i, d],
                recv_sem=part_recv.at[i, d],
                device_id={"rep": lax.rem(rep + d, reps)},
                device_id_type=MESH,
            )
            copy.start()
            copies.append(copy)
        return copies

    def set_coefs(z, before, after):
        left_rows = jnp.concatenate([before, z[: rows - 1]], axis=0)
        right_rows = jnp.concatenate([z[1:], after], axis=0)
        left = jnp.where(lane == 0, pltpu.roll(left_rows, 1, 1), pltpu.roll(z, 1, 1))
        right = jnp.where(
            lane == LANES - 1,
            pltpu.roll(right_rows, LANES - 1, 1),
            pltpu.roll(z, LANES - 1, 1),
        )
        slope = 0.5 * (right - left)
        bend = 0.5 * (right - 2.0 * z + left)
        coefs[0] = scale * z
        coefs[1] = scale * slope
        coefs[2] = scale * bend
        coefs[3] = scale * (z - slope * edge + bend * edge * edge)
        coefs[4] = scale * (z + slope * edge + bend * edge * edge)
        return noise_sum[...] + cells * z + square_sum * bend

    def burst(i, g, unused):
        centre, slope, bend = row(0, g), row(1, g), row(2, g)
        ghost_left, ghost_right = row(3, g), row(4, g)
        kap, mid, top = row(5, g), row(6, g), row(7, g)
        base = centre + first_place * (slope + bend * first_place)
        tilt = slope + 2.0 * first_place * bend
        state = []
        for k in range(depth):
            shift = k / cells
            if k == 0:
                state.append(base + noise[g, k])
            else:
                state.append(base + shift * (tilt + shift * bend) + noise[g, k])
        for step in range(STEPS - 1):
            below = jnp.where(sub == 0, ghost_left, pltpu.roll(state[-1], 1, 0))
            above = jnp.where(sub == SUB - 1, ghost_right, pltpu.roll(state[0], SUB - 1, 0))
            padded = [below] + state + [above]
            state = [
                padded[k + 1] * (mid - padded[k + 1] * padded[k + 1])
                + kap * (padded[k] + padded[k + 2])
                for k in range(depth)
            ]
        sums = []
        for w in state:
            sums.append(w * (top - w * w))
        while len(sums) > 1:
            sums = [sums[t] + sums[t + 1] for t in range(0, len(sums), 2)]
        ends = jnp.where(sub == 0, ghost_left - state[0], 0.0) + jnp.where(
            sub == SUB - 1, ghost_right - state[-1], 0.0
        )
        grown = jnp.sum(sums[0] + kap * ends, axis=0, keepdims=True)
        parts[i, rep, pl.ds(g, 1), :] = grown * coefs[8, pl.ds(g, 1), :]
        return unused

    def bursts(i, indices):
        if len(indices) == 1:
            burst(i, indices[0], 0)
        else:
            stride = indices[1] - indices[0]
            lax.fori_loop(
                0, len(indices), lambda t, c: burst(i, indices[0] + t * stride, c), 0
            )

    def finish(i, start_sum, pending):
        parts[i, rep] = parts[i, rep] - start_sum
        copies = send_parts(i)
        for copy in pending:
            copy.wait_send()
        for copy in copies:
            copy.wait_recv()
        acc = parts[i, 0]
        for q in range(1, reps):
            acc = acc + parts[i, q]
        return acc * amplitude, copies

    has_left = me > 0
    has_right = me < macros - 1

    def outside(before, after):
        return (
            jnp.where(has_left, before, 0.0),
            jnp.where(has_right, after, 0.0),
        )

    def drift(i, z, before, after, pending):
        start_sum = set_coefs(z, *outside(before, after))
        bursts(i, list(range(rows)))
        return finish(i, start_sum, pending)

    sides = [1, macros - 1] if macros > 2 else [1]
    others = list(range(1, macros))

    def edges(r):
        return whole[r, macros - 1, rows - 1 : rows, :], whole[r, 1, 0:1, :]

    u_old = u_ref[...]
    old_copies = send_whole(0, u_ref, sides)
    nothing = jnp.zeros((1, LANES), jnp.float32)
    if rows > 2:
        set_coefs(u_old, nothing, nothing)
        bursts(0, list(range(1, rows - 1)))
    for copy in old_copies:
        copy.wait_recv()
    start_sum = set_coefs(u_old, *outside(*edges(0)))
    bursts(0, [0, rows - 1] if rows > 2 else list(range(rows)))
    f_old, sent_parts = finish(0, start_sum, old_copies)

    u_start = u_old + proj_step * f_old
    whole[1, 0] = u_start
    copies = send_whole(1, whole.at[1, 0], sides)
    for copy in sent_parts:
        copy.wait_send()
    for copy in copies:
        copy.wait_recv()
    u_before, u_after = edges(1)
    f_start, sent_parts = drift(1, u_start, u_before, u_after, copies)
    resid = -(u_start - u_old - proj_step * f_start)

    def gather(r, value, sent):
        whole[r, 0] = value
        copies = send_whole(r, whole.at[r, 0], others)
        for copy in sent:
            copy.wait_send()
        for copy in copies:
            copy.wait_recv()
        return whole[r].reshape(macros * rows, LANES), copies

    flat, copies = gather(2, resid, sent_parts)
    beta = jnp.sqrt(total(flat * flat))
    basis = [flat / beta]
    givens = Givens(beta)
    for j in range(ITERS):
        probe = basis[j]
        before = probe[macros * rows - 1 : macros * rows]
        after = probe[rows : rows + 1]
        f_probe, sent_parts = drift(
            j + 2,
            u_start + delta * probe[:rows],
            u_before + delta * before,
            u_after + delta * after,
            copies,
        )
        image = probe[:rows] - proj_step * (f_probe - f_start) / delta
        flat, copies = gather(j + 3, image, sent_parts)
        column = [total(vector * flat) for vector in basis]
        for coeff, vector in zip(column, basis):
            flat = flat - coeff * vector
        length = jnp.sqrt(total(flat * flat))
        column.append(length)
        givens.add(column)
        if j + 1 < ITERS:
            basis.append(flat / length)
    for copy in copies:
        copy.wait_send()
    result = u_start
    for coeff, vector in zip(givens.solve(), basis):
        result = result + coeff * vector[:rows]
    out_ref[...] = result


def solution(mesh):
    macros, reps = mesh.shape["macro"], mesh.shape["rep"]

    def step(u_old, rate, kappa, seed):
        local = u_old.shape[0]
        cells = seed.shape[2]
        rows = local // LANES
        depth = cells // SUB
        shape = (rows, LANES)
        vmem = pl.BlockSpec(memory_space=pltpu.VMEM)
        out = pl.pallas_call(
            functools.partial(kernel, macros, reps * seed.shape[0], cells, rows),
            out_shape=jax.ShapeDtypeStruct(shape, jnp.float32),
            in_specs=[vmem, vmem, vmem, pl.BlockSpec(memory_space=pl.ANY)],
            out_specs=vmem,
            scratch_shapes=[
                pltpu.VMEM((rows, LANES, cells), jnp.int32),
                pltpu.VMEM((SUB * (depth + 8), LANES), jnp.float32),
                pltpu.VMEM((rows, depth, SUB, LANES), jnp.float32),
                pltpu.VMEM(shape, jnp.float32),
                pltpu.VMEM((10,) + shape, jnp.float32),
                pltpu.VMEM((ITERS + 2, reps) + shape, jnp.float32),
                pltpu.VMEM((ITERS + 3, macros) + shape, jnp.float32),
                pltpu.SemaphoreType.DMA((rows,)),
                pltpu.SemaphoreType.DMA((ITERS + 2, reps)),
                pltpu.SemaphoreType.DMA((ITERS + 2, reps)),
                pltpu.SemaphoreType.DMA((ITERS + 3, macros)),
                pltpu.SemaphoreType.DMA((ITERS + 3, macros)),
            ],
            compiler_params=pltpu.CompilerParams(collective_id=0, has_side_effects=True),
        )(u_old.reshape(shape), rate.reshape(shape), kappa.reshape(shape), seed)
        return out.reshape(local)

    placed = (P("macro"), P("macro"), P("macro"), P("rep", "macro", None))
    return jax.shard_map(step, mesh=mesh, in_specs=placed, out_specs=P("macro"), check_vma=False)
```

time: 278 us -> 59.4 us (0.21)
  blocking collectives: 139 us -> 0 us
  Pallas kernels: 0 us -> 58 us
  other arithmetic: 49.8 us -> 0 us
  starting transfers between devices: 39.4 us -> 0 us
  local copies, waits for them, and re-layouts: 22.8 us -> 1.26 us
  between operations: 21.2 us -> 0.01 us
  waiting for transfers between devices: 4.81 us -> 0 us
    psum x11 -> x0, blocking collectives: 139 us -> none  [the longest x5 104 us: inner(): return lax.psum(values, 'macro')]
    pallas_call x0 -> x1, Pallas kernels: none -> 58 us  [step(): pl.pallas_call(functools.partial(kernel, macros, reps * seed.shape[0], ce...]
    ppermute x12 -> x0, starting transfers between devices: 39.4 us -> none  [the longest x6 31.6 us: with_halo(): lax.ppermute(tail, axis, [(i, (i + 1) % count) for i in range(ends)])]
    add x60 -> x0, other arithmetic: 26.4 us -> none  [the longest x42 18.7 us: ensemble_aggregate(): state + kappa * (upper + lower - 2.0 * state)]
    slice x58 -> x0, local copies, waits for them, and re-layouts: 17.1 us -> none  [the longest x48 9.65 us: ensemble_aggregate(): lower = jnp.concatenate([left_col, state[:, :, :-1]], axis=2)]
    reduce_sum x14 -> x0, other arithmetic: 9.83 us -> none  [the longest x6 4.54 us: ensemble_aggregate(): return jnp.sum(state - start, axis=(0, 2))]
    concatenate x6 -> x0, other arithmetic: 7.59 us -> none  [with_halo(): jnp.concatenate([lax.ppermute(tail, axis, [(i, (i + 1) % count) for i in...]
    another operation x3 -> x0, other arithmetic: 5.98 us -> none  [per_device(): dots = inner(jnp.stack(pieces))]
  transfers between devices with their start and end apart: 12 -> 0, of which waited for: 6 -> 0; matrix products, arithmetic and copies ran while one was open for 0% -> 0% of each run, Pallas kernels for 0% -> 0%
where the time goes in v1:
time: 59.4 us; the launch traced here: 59.3 us
  Pallas kernels  58 us (98%)
  local copies, waits for them, and re-layouts  1.26 us (2%)
    pallas_call x1, Pallas kernels, step(): pl.pallas_call(functools.partial(kernel, macros, reps * seed.shape[0], ce...  58 us
    unnamed x1, local copies, waits for them, and re-layouts  1.26 us

profile of v1, /device:TPU:0, one launch (start us, length us, event | category | flops | bytes accessed | tf_op | source)
XLA Modules:
  0.0 59.3 jit_solution(460867217472433255)
XLA Ops:
  0.0 58.0 %shard_map.46 = f32[4,128]{1,0:T(4,128)} custom-call(f32[4,128]{1,0:T(4,128)} %bitcast.5, f32[4,128]{1,0:T(4,128)} %bitcast.6, f32[4,128]{1,0:T(4,128)} %bitcast.7, s32[1,512,256]{2,1,0:T(8,128)} %seed_ref.1), custom_call_target="tpu_custom_call" | custom-call | tf_op jit(solution)/shard_map/pallas_call | solution.py:353
  58.0 1.3 %copy.6 = f32[512]{0:T(512)} copy(f32[512]{0:T(512)} %bitcast.4) | data formatting | bytes 4096

commit v2 on v1

--- a/solution.py
+++ b/solution.py
@@ -23,7 +23,8 @@
 
 
 def total(values):
-    return jnp.sum(jnp.sum(values, axis=0, keepdims=True), axis=1, keepdims=True)
+    folded = jnp.sum(values, axis=0, keepdims=True)
+    return jnp.sum(jnp.sum(folded, axis=1, keepdims=True), axis=2, keepdims=True)
 
 
 class Givens:
@@ -78,12 +79,12 @@
     noise_sum,
     coefs,
     parts,
-    whole,
+    olds,
     load_sem,
+    old_send,
+    old_recv,
     part_send,
     part_recv,
-    whole_send,
-    whole_recv,
 ):
     depth = cells // SUB
     pitch = flipped.shape[0] // SUB
@@ -103,14 +104,14 @@
         load.start()
 
     barrier = pltpu.get_barrier_semaphore()
-    for d in range(1, macros):
-        pl.semaphore_signal(
-            barrier, inc=1, device_id={"macro": lax.rem(me + d, macros)}, device_id_type=MESH
-        )
-    for d in range(1, reps):
-        pl.semaphore_signal(
-            barrier, inc=1, device_id={"rep": lax.rem(rep + d, reps)}, device_id_type=MESH
-        )
+    peers = [(d, e) for d in range(macros) for e in range(reps)][1:]
+
+    def peer(d, e):
+        macro = me if d == 0 else lax.rem(me + (macros - d), macros)
+        return {"macro": macro, "rep": rep if e == 0 else lax.rem(rep + e, reps)}
+
+    for d, e in peers:
+        pl.semaphore_signal(barrier, inc=1, device_id=peer(d, e), device_id_type=MESH)
 
     growth = micro_dt * rate_ref[...]
     scale = jnp.sqrt(growth)
@@ -143,7 +144,7 @@
 
     lax.fori_loop(0, rows, prepare, 0)
 
-    pl.semaphore_wait(barrier, macros - 1 + reps - 1)
+    pl.semaphore_wait(barrier, len(peers))
 
     lane = lax.broadcasted_iota(jnp.int32, (rows, LANES), 1)
     sub = lax.broadcasted_iota(jnp.int32, (SUB, LANES), 0)
@@ -152,35 +153,25 @@
     first_place = sub.astype(jnp.float32) * (depth / cells) + (0.5 / cells - 0.5)
     edge = 0.5 + 0.5 / cells
 
-    def send_whole(r, source, ds):
-        copies = []
-        for d in ds:
-            copy = pltpu.make_async_remote_copy(
-                src_ref=source,
-                dst_ref=whole.at[r, d],
-                send_sem=whole_send.at[r, d],
-                recv_sem=whole_recv.at[r, d],
-                device_id={"macro": lax.rem(me + (macros - d), macros)},
+    def send_parts(i):
+        own = parts.at[i, rep]
+        for d, e in peers:
+            pltpu.make_async_remote_copy(
+                src_ref=own,
+                dst_ref=parts.at[i, d * reps + rep],
+                send_sem=part_send.at[i],
+                recv_sem=part_recv.at[i],
+                device_id=peer(d, e),
                 device_id_type=MESH,
-            )
-            copy.start()
-            copies.append(copy)
-        return copies
-
-    def send_parts(i):
-        copies = []
-        for d in range(1, reps):
-            copy = pltpu.make_async_remote_copy(
-                src_ref=parts.at[i, rep],
-                dst_ref=parts.at[i, rep],
-                send_sem=part_send.at[i, d],
-                recv_sem=part_recv.at[i, d],
-                device_id={"rep": lax.rem(rep + d, reps)},
-                device_id_type=MESH,
-            )
-            copy.start()
-            copies.append(copy)
-        return copies
+            ).start()
+
+    def all_sent(i):
+        sent = parts.at[i, pl.ds(1, len(peers))]
+        pltpu.make_async_copy(sent, sent, part_send.at[i]).wait()
+
+    def all_received(i):
+        got = parts.at[i, pl.ds(1, len(peers))]
+        pltpu.make_async_copy(got, got, part_recv.at[i]).wait()
 
     def set_coefs(z, before, after):
         left_rows = jnp.concatenate([before, z[: rows - 1]], axis=0)
@@ -198,7 +189,7 @@
         coefs[2] = scale * bend
         coefs[3] = scale * (z - slope * edge + bend * edge * edge)
         coefs[4] = scale * (z + slope * edge + bend * edge * edge)
-        return noise_sum[...] + cells * z + square_sum * bend
+        coefs[10] = noise_sum[...] + cells * z + square_sum * bend
 
     def burst(i, g, unused):
         centre, slope, bend = row(0, g), row(1, g), row(2, g)
@@ -231,7 +222,8 @@
             sub == SUB - 1, ghost_right - state[-1], 0.0
         )
         grown = jnp.sum(sums[0] + kap * ends, axis=0, keepdims=True)
-        parts[i, rep, pl.ds(g, 1), :] = grown * coefs[8, pl.ds(g, 1), :]
+        change = grown * coefs[8, pl.ds(g, 1), :] - coefs[10, pl.ds(g, 1), :]
+        parts[i, rep, pl.ds(g, 1), :] = change
         return unused
 
     def bursts(i, indices):
@@ -243,17 +235,16 @@
                 0, len(indices), lambda t, c: burst(i, indices[0] + t * stride, c), 0
             )
 
-    def finish(i, start_sum, pending):
-        parts[i, rep] = parts[i, rep] - start_sum
-        copies = send_parts(i)
-        for copy in pending:
-            copy.wait_send()
-        for copy in copies:
-            copy.wait_recv()
-        acc = parts[i, 0]
+    def finish(i):
+        send_parts(i)
+        if i:
+            all_sent(i - 1)
+        all_received(i)
+        every = parts[i].reshape(macros, reps, rows, LANES)
+        acc = every[:, 0]
         for q in range(1, reps):
-            acc = acc + parts[i, q]
-        return acc * amplitude, copies
+            acc = acc + every[:, q]
+        return acc * amplitude
 
     has_left = me > 0
     has_right = me < macros - 1
@@ -264,79 +255,61 @@
             jnp.where(has_right, after, 0.0),
         )
 
-    def drift(i, z, before, after, pending):
-        start_sum = set_coefs(z, *outside(before, after))
+    def edges(field):
+        return field[macros - 1, rows - 1 : rows, :], field[1, 0:1, :]
+
+    def drift(i, field):
+        set_coefs(field[0], *outside(*edges(field)))
         bursts(i, list(range(rows)))
-        return finish(i, start_sum, pending)
-
-    sides = [1, macros - 1] if macros > 2 else [1]
-    others = list(range(1, macros))
-
-    def edges(r):
-        return whole[r, macros - 1, rows - 1 : rows, :], whole[r, 1, 0:1, :]
-
-    u_old = u_ref[...]
-    old_copies = send_whole(0, u_ref, sides)
+        return finish(i)
+
+    copies = []
+    for d in range(1, macros):
+        copy = pltpu.make_async_remote_copy(
+            src_ref=u_ref,
+            dst_ref=olds.at[d],
+            send_sem=old_send.at[d],
+            recv_sem=old_recv.at[d],
+            device_id=peer(d, 0),
+            device_id_type=MESH,
+        )
+        copy.start()
+        copies.append(copy)
+    own = u_ref[...]
+    olds[0] = own
     nothing = jnp.zeros((1, LANES), jnp.float32)
     if rows > 2:
-        set_coefs(u_old, nothing, nothing)
+        set_coefs(own, nothing, nothing)
         bursts(0, list(range(1, rows - 1)))
-    for copy in old_copies:
-        copy.wait_recv()
-    start_sum = set_coefs(u_old, *outside(*edges(0)))
+    for copy in copies:
+        copy.wait()
+    u_old = olds[...]
+    set_coefs(own, *outside(*edges(u_old)))
     bursts(0, [0, rows - 1] if rows > 2 else list(range(rows)))
-    f_old, sent_parts = finish(0, start_sum, old_copies)
+    f_old = finish(0)
 
     u_start = u_old + proj_step * f_old
-    whole[1, 0] = u_start
-    copies = send_whole(1, whole.at[1, 0], sides)
-    for copy in sent_parts:
-        copy.wait_send()
-    for copy in copies:
-        copy.wait_recv()
-    u_before, u_after = edges(1)
-    f_start, sent_parts = drift(1, u_start, u_before, u_after, copies)
+    f_start = drift(1, u_start)
     resid = -(u_start - u_old - proj_step * f_start)
-
-    def gather(r, value, sent):
-        whole[r, 0] = value
-        copies = send_whole(r, whole.at[r, 0], others)
-        for copy in sent:
-            copy.wait_send()
-        for copy in copies:
-            copy.wait_recv()
-        return whole[r].reshape(macros * rows, LANES), copies
-
-    flat, copies = gather(2, resid, sent_parts)
-    beta = jnp.sqrt(total(flat * flat))
-    basis = [flat / beta]
+    beta = jnp.sqrt(total(resid * resid))
+    basis = [resid / beta]
     givens = Givens(beta)
     for j in range(ITERS):
         probe = basis[j]
-        before = probe[macros * rows - 1 : macros * rows]
-        after = probe[rows : rows + 1]
-        f_probe, sent_parts = drift(
-            j + 2,
-            u_start + delta * probe[:rows],
-            u_before + delta * before,
-            u_after + delta * after,
-            copies,
-        )
-        image = probe[:rows] - proj_step * (f_probe - f_start) / delta
-        flat, copies = gather(j + 3, image, sent_parts)
-        column = [total(vector * flat) for vector in basis]
+        f_probe = drift(j + 2, u_start + delta * probe)
+        image = probe - proj_step * (f_probe - f_start) / delta
+        column = [total(vector * image) for vector in basis]
         for coeff, vector in zip(column, basis):
-            flat = flat - coeff * vector
-        length = jnp.sqrt(total(flat * flat))
+            image = image - coeff * vector
+        length = jnp.sqrt(total(image * image))
         column.append(length)
         givens.add(column)
         if j + 1 < ITERS:
-            basis.append(flat / length)
-    for copy in copies:
-        copy.wait_send()
-    result = u_start
+            basis.append(image / length)
+    all_sent(ITERS + 1)
+    result = u_start[0]
     for coeff, vector in zip(givens.solve(), basis):
-        result = result + coeff * vector[:rows]
+        result = result + coeff[0] * vector[0]
     out_ref[...] = result
 
 
@@ -360,14 +333,14 @@
                 pltpu.VMEM((SUB * (depth + 8), LANES), jnp.float32),
                 pltpu.VMEM((rows, depth, SUB, LANES), jnp.float32),
                 pltpu.VMEM(shape, jnp.float32),
-                pltpu.VMEM((10,) + shape, jnp.float32),
-                pltpu.VMEM((ITERS + 2, reps) + shape, jnp.float32),
-                pltpu.VMEM((ITERS + 3, macros) + shape, jnp.float32),
+                pltpu.VMEM((11,) + shape, jnp.float32),
+                pltpu.VMEM((ITERS + 2, macros * reps) + shape, jnp.float32),
+                pltpu.VMEM((macros,) + shape, jnp.float32),
                 pltpu.SemaphoreType.DMA((rows,)),
-                pltpu.SemaphoreType.DMA((ITERS + 2, reps)),
-                pltpu.SemaphoreType.DMA((ITERS + 2, reps)),
-                pltpu.SemaphoreType.DMA((ITERS + 3, macros)),
-                pltpu.SemaphoreType.DMA((ITERS + 3, macros)),
+                pltpu.SemaphoreType.DMA((macros,)),
+                pltpu.SemaphoreType.DMA((macros,)),
+                pltpu.SemaphoreType.DMA((ITERS + 2,)),
+                pltpu.SemaphoreType.DMA((ITERS + 2,)),
             ],
             compiler_params=pltpu.CompilerParams(collective_id=0, has_side_effects=True),
         )(u_old.reshape(shape), rate.reshape(shape), kappa.reshape(shape), seed)

time: 59.4 us -> 47.9 us (0.81)
  Pallas kernels: 58 us -> 46.5 us
    pallas_call x1, Pallas kernels: 58 us -> 46.5 us  [step(): pl.pallas_call(functools.partial(kernel, macros, reps * seed.shape[0], ce...]
where the time goes in v2:
time: 47.9 us; the launch traced here: 47.7 us
  Pallas kernels  46.5 us (97%)
  local copies, waits for them, and re-layouts  1.26 us (3%)
    pallas_call x1, Pallas kernels, step(): pl.pallas_call(functools.partial(kernel, macros, reps * seed.shape[0], ce...  46.5 us
    unnamed x1, local copies, waits for them, and re-layouts  1.26 us

profile of v2, /device:TPU:0, one launch (start us, length us, event | category | flops | bytes accessed | tf_op | source)
XLA Modules:
  0.0 47.7 jit_solution(15581063747200552257)
XLA Ops:
  0.0 46.5 %shard_map.46 = f32[4,128]{1,0:T(4,128)} custom-call(f32[4,128]{1,0:T(4,128)} %bitcast.5, f32[4,128]{1,0:T(4,128)} %bitcast.6, f32[4,128]{1,0:T(4,128)} %bitcast.7, s32[1,512,256]{2,1,0:T(8,128)} %seed_ref.1), custom_call_target="tpu_custom_call" | custom-call | tf_op jit(solution)/shard_map/pallas_call | solution.py:326
  46.5 1.3 %copy.6 = f32[512]{0:T(512)} copy(f32[512]{0:T(512)} %bitcast.4) | data formatting | bytes 4096

commit v3 on v2

--- a/solution.py
+++ b/solution.py
@@ -68,11 +68,15 @@
     reps,
     cells,
     rows,
+    u_in,
+    rate_in,
+    kappa_in,
+    seed_ref,
+    out_ref,
     u_ref,
     rate_ref,
     kappa_ref,
-    seed_ref,
-    out_ref,
+    edge_ref,
     raw,
     flipped,
     noise,
@@ -81,10 +85,12 @@
     parts,
     olds,
     load_sem,
+    small_sem,
     old_send,
     old_recv,
     part_send,
     part_recv,
+    near_recv,
 ):
     depth = cells // SUB
     pitch = flipped.shape[0] // SUB
@@ -100,7 +106,13 @@
         )
         for g in range(rows)
     ]
-    for load in loads:
+    small = [
+        pltpu.make_async_copy(source, target, small_sem.at[t])
+        for t, (source, target) in enumerate(
+            [(rate_in, rate_ref), (kappa_in, kappa_ref), (u_in, u_ref)]
+        )
+    ]
+    for load in small + loads:
         load.start()
 
     barrier = pltpu.get_barrier_semaphore()
@@ -113,6 +125,8 @@
     for d, e in peers:
         pl.semaphore_signal(barrier, inc=1, device_id=peer(d, e), device_id_type=MESH)
 
+    for load in small:
+        load.wait()
     growth = micro_dt * rate_ref[...]
     scale = jnp.sqrt(growth)
     kappa = kappa_ref[...]
@@ -153,6 +167,8 @@
     first_place = sub.astype(jnp.float32) * (depth / cells) + (0.5 / cells - 0.5)
     edge = 0.5 + 0.5 / cells
 
+    near = {0: near_recv.at[0], 1: near_recv.at[1], macros - 1: near_recv.at[2]}
+
     def send_parts(i):
         own = parts.at[i, rep]
         for d, e in peers:
@@ -160,7 +176,7 @@
                 src_ref=own,
                 dst_ref=parts.at[i, d * reps + rep],
                 send_sem=part_send.at[i],
-                recv_sem=part_recv.at[i],
+                recv_sem=part_recv.at[i] if i else near.get(d, part_recv.at[0]),
                 device_id=peer(d, e),
                 device_id_type=MESH,
             ).start()
@@ -168,6 +184,14 @@
     def all_sent(i):
         sent = parts.at[i, pl.ds(1, len(peers))]
         pltpu.make_async_copy(sent, sent, part_send.at[i]).wait()
+
+    def near_received(d):
+        got = parts.at[0, pl.ds(1, reps - 1) if d == 0 else pl.ds(d * reps, reps)]
+        pltpu.make_async_copy(got, got, near[d]).wait()
+
+    def far_received():
+        got = parts.at[0, pl.ds(2 * reps, (macros - 3) * reps)]
+        pltpu.make_async_copy(got, got, part_recv.at[0]).wait()
 
     def all_received(i):
         got = parts.at[i, pl.ds(1, len(peers))]
@@ -235,17 +259,19 @@
                 0, len(indices), lambda t, c: burst(i, indices[0] + t * stride, c), 0
             )
 
-    def finish(i):
-        send_parts(i)
-        if i:
-            all_sent(i - 1)
-        all_received(i)
+    def summed(i):
         every = parts[i].reshape(macros, reps, rows, LANES)
         acc = every[:, 0]
         for q in range(1, reps):
             acc = acc + every[:, q]
         return acc * amplitude
 
+    def summed_block(d, first, last):
+        acc = parts[0, d * reps, first:last, :]
+        for q in range(1, reps):
+            acc = acc + parts[0, d * reps + q, first:last, :]
+        return acc * amplitude
+
     has_left = me > 0
     has_right = me < macros - 1
 
@@ -261,7 +287,10 @@
     def drift(i, field):
         set_coefs(field[0], *outside(*edges(field)))
         bursts(i, list(range(rows)))
-        return finish(i)
+        send_parts(i)
+        all_sent(i - 1)
+        all_received(i)
+        return summed(i)
 
     copies = []
     for d in range(1, macros):
@@ -281,15 +310,59 @@
     if rows > 2:
         set_coefs(own, nothing, nothing)
         bursts(0, list(range(1, rows - 1)))
+    right_copy, left_copy = copies[0], copies[-1]
+    edge_ref[...] = jnp.zeros_like(edge_ref)
+
+    @pl.when(has_left)
+    def _():
+        left_copy.wait_recv()
+        edge_ref[0] = olds[macros - 1, rows - 1 : rows, :]
+
+    @pl.when(has_right)
+    def _():
+        right_copy.wait_recv()
+        edge_ref[1] = olds[1, 0:1, :]
+
+    set_coefs(own, edge_ref[0], edge_ref[1])
+    bursts(0, [0, rows - 1] if rows > 2 else list(range(rows)))
+    send_parts(0)
+    near_received(0)
+
+    @pl.when(has_left)
+    def _():
+        near_received(macros - 1)
+        edge_ref[0] = edge_ref[0] + proj_step * summed_block(macros - 1, rows - 1, rows)
+
+    @pl.when(has_right)
+    def _():
+        near_received(1)
+        edge_ref[1] = edge_ref[1] + proj_step * summed_block(1, 0, 1)
+
+    set_coefs(own + proj_step * summed_block(0, 0, rows), edge_ref[0], edge_ref[1])
+    bursts(1, list(range(rows)))
+    send_parts(1)
+
+    @pl.when(jnp.logical_not(has_left))
+    def _():
+        left_copy.wait_recv()
+        near_received(macros - 1)
+
+    @pl.when(jnp.logical_not(has_right))
+    def _():
+        right_copy.wait_recv()
+        near_received(1)
+
+    for copy in copies[1:-1]:
+        copy.wait_recv()
     for copy in copies:
-        copy.wait()
+        copy.wait_send()
+    far_received()
+    all_sent(0)
     u_old = olds[...]
-    set_coefs(own, *outside(*edges(u_old)))
-    bursts(0, [0, rows - 1] if rows > 2 else list(range(rows)))
-    f_old = finish(0)
-
+    f_old = summed(0)
     u_start = u_old + proj_step * f_old
-    f_start = drift(1, u_start)
+    all_received(1)
+    f_start = summed(1)
     resid = -(u_start - u_old - proj_step * f_start)
     beta = jnp.sqrt(total(resid * resid))
     basis = [resid / beta]
@@ -325,10 +398,14 @@
         vmem = pl.BlockSpec(memory_space=pltpu.VMEM)
         out = pl.pallas_call(
             functools.partial(kernel, macros, reps * seed.shape[0], cells, rows),
-            out_shape=jax.ShapeDtypeStruct(shape, jnp.float32),
-            in_specs=[vmem, vmem, vmem, pl.BlockSpec(memory_space=pl.ANY)],
+            out_shape=pltpu.VMEM(shape, jnp.float32),
+            in_specs=[pl.BlockSpec(memory_space=pl.ANY)] * 4,
             out_specs=vmem,
             scratch_shapes=[
+                pltpu.VMEM(shape, jnp.float32),
+                pltpu.VMEM(shape, jnp.float32),
+                pltpu.VMEM(shape, jnp.float32),
+                pltpu.VMEM((2, 1, LANES), jnp.float32),
                 pltpu.VMEM((rows, LANES, cells), jnp.int32),
                 pltpu.VMEM((SUB * (depth + 8), LANES), jnp.float32),
                 pltpu.VMEM((rows, depth, SUB, LANES), jnp.float32),
@@ -337,10 +414,12 @@
                 pltpu.VMEM((ITERS + 2, macros * reps) + shape, jnp.float32),
                 pltpu.VMEM((macros,) + shape, jnp.float32),
                 pltpu.SemaphoreType.DMA((rows,)),
+                pltpu.SemaphoreType.DMA((3,)),
                 pltpu.SemaphoreType.DMA((macros,)),
                 pltpu.SemaphoreType.DMA((macros,)),
                 pltpu.SemaphoreType.DMA((ITERS + 2,)),
                 pltpu.SemaphoreType.DMA((ITERS + 2,)),
+                pltpu.SemaphoreType.DMA((3,)),
             ],
             compiler_params=pltpu.CompilerParams(collective_id=0, has_side_effects=True),
         )(u_old.reshape(shape), rate.reshape(shape), kappa.reshape(shape), seed)

time: 47.9 us -> 43.9 us (0.916)
  Pallas kernels: 46.5 us -> 43.1 us
  local copies, waits for them, and re-layouts: 1.26 us -> 0.58 us
    pallas_call x1, Pallas kernels: 46.5 us -> 43.1 us  [step(): pl.pallas_call(functools.partial(kernel, macros, reps * seed.shape[0], ce...]
    unnamed x1, local copies, waits for them, and re-layouts: 1.26 us -> 0.58 us
where the time goes in v3:
time: 43.9 us; the launch traced here: 43.7 us
  Pallas kernels  43.1 us (98%)
  local copies, waits for them, and re-layouts  0.58 us (1%)
    pallas_call x1, Pallas kernels, step(): pl.pallas_call(functools.partial(kernel, macros, reps * seed.shape[0], ce...  43.1 us

profile of v3, /device:TPU:0, one launch (start us, length us, event | category | flops | bytes accessed | tf_op | source)
XLA Modules:
  0.0 43.7 jit_solution(14734640465588900421)
XLA Ops:
  0.0 43.1 %shard_map.46 = f32[4,128]{1,0:T(4,128)S(1)} custom-call(f32[4,128]{1,0:T(4,128)} %bitcast.5, f32[4,128]{1,0:T(4,128)} %bitcast.6, f32[4,128]{1,0:T(4,128)} %bitcast.7, s32[1,512,256]{2,1,0:T(8,128)} %seed_ref.1), custom_call_target="tpu_custom_call" | custom-call | tf_op jit(solution)/shard_map/pallas_call | solution.py:399
  43.1 0.6 %copy.6 = f32[512]{0:T(512)} copy(f32[512]{0:T(512)S(1)} %bitcast.4) | data formatting | bytes 4096

commit v4 on v3

--- a/solution.py
+++ b/solution.py
@@ -112,9 +112,6 @@
             [(rate_in, rate_ref), (kappa_in, kappa_ref), (u_in, u_ref)]
         )
     ]
-    for load in small + loads:
-        load.start()
-
     barrier = pltpu.get_barrier_semaphore()
     peers = [(d, e) for d in range(macros) for e in range(reps)][1:]
 
@@ -125,6 +122,8 @@
     for d, e in peers:
         pl.semaphore_signal(barrier, inc=1, device_id=peer(d, e), device_id_type=MESH)
 
+    for load in small + loads:
+        load.start()
     for load in small:
         load.wait()
     growth = micro_dt * rate_ref[...]
@@ -169,9 +168,11 @@
 
     near = {0: near_recv.at[0], 1: near_recv.at[1], macros - 1: near_recv.at[2]}
 
+    far_first = sorted(peers, key=lambda p: (abs(p[1] - reps // 2), -(p[0] % 2), -abs(p[0] - macros / 2)))
+
     def send_parts(i):
         own = parts.at[i, rep]
-        for d, e in peers:
+        for d, e in far_first:
             pltpu.make_async_remote_copy(
                 src_ref=own,
                 dst_ref=parts.at[i, d * reps + rep],

time: 43.9 us -> 42 us (0.957)
  Pallas kernels: 43.1 us -> 41.2 us
    pallas_call x1, Pallas kernels: 43.1 us -> 41.2 us  [step(): pl.pallas_call(functools.partial(kernel, macros, reps * seed.shape[0], ce...]
where the time goes in v4:
time: 42 us; the launch traced here: 41.8 us
  Pallas kernels  41.2 us (98%)
  local copies, waits for them, and re-layouts  0.58 us (1%)
    pallas_call x1, Pallas kernels, step(): pl.pallas_call(functools.partial(kernel, macros, reps * seed.shape[0], ce...  41.2 us

profile of v4, /device:TPU:0, one launch (start us, length us, event | category | flops | bytes accessed | tf_op | source)
XLA Modules:
  0.0 41.8 jit_solution(2319867570976287886)
XLA Ops:
  0.0 41.2 %shard_map.46 = f32[4,128]{1,0:T(4,128)S(1)} custom-call(f32[4,128]{1,0:T(4,128)} %bitcast.5, f32[4,128]{1,0:T(4,128)} %bitcast.6, f32[4,128]{1,0:T(4,128)} %bitcast.7, s32[1,512,256]{2,1,0:T(8,128)} %seed_ref.1), custom_call_target="tpu_custom_call" | custom-call | tf_op jit(solution)/shard_map/pallas_call | solution.py:400
  41.2 0.6 %copy.6 = f32[512]{0:T(512)} copy(f32[512]{0:T(512)S(1)} %bitcast.4) | data formatting | bytes 4096
